TPU v7x, 32 devices: a whole 2x2x4 slice. The times are simulated.
32 devices in a mesh: section: 4 (over y, x), tp: 8 (over z, core).
Axes of the slice: x: 2, y: 2, z: 4, core: 2. Of those that a mesh axis runs over, the one named last changes fastest.
Arguments:
- awaiting_arrivals: bfloat16 [4, 8, 25, 1920], P('section', 'tp'), may hold values from -6 to 6
- label_numbers: int32 [5, 8], replicated, may hold values from 0 to 1000
- drawn_coarse_codes: int32 [1, 8, 30], replicated, may hold values from 0 to 4095
- discrete_prototypes: float32 [4096, 32], replicated, may hold values from -6 to 6
- code_raising_operator: bfloat16 [32, 1920], replicated, may hold values from -1 to 1
- placement_tier_features: bfloat16 [25, 1920], replicated, may hold values from -3 to 3
- label_feature_rows: bfloat16 [1001, 1920], P(None, 'tp'), may hold values from -6 to 6
- conditioned_gain_mapping: bfloat16 [4, 1920, 3, 1920], P('section', None, None, 'tp'), may hold values from -0.125 to 0.125
- conditioned_shift_addend: float32 [4, 3, 1920], P('section', None, 'tp'), may hold values from -3 to 3
- question_answer_operator: bfloat16 [4, 1920, 3, 1920], P('section', None, None, 'tp'), may hold values from -0.125 to 0.125
- mixing_return_operator: bfloat16 [4, 1920, 1920], P('section', None, 'tp'), may hold values from -0.125 to 0.125
- focus_sharpness_exponents: float32 [4, 30], P('section'), may hold values from 1 to 5.5
- prior_resolution_probes: bfloat16 [4, 2, 8, 30, 1920], P('section', None, 'tp'), may hold values from -0.75 to 0.75
- prior_resolution_answers: bfloat16 [4, 2, 8, 30, 1920], P('section', None, 'tp'), may hold values from -6 to 6
Outputs:
- section_out: bfloat16 [4, 2, 8, 25, 1920], P('section', None, 'tp')
Inputs may be any that keep to these rules, and one draw needn't show every extreme that they name: `drawn_coarse_codes`: codebook indices of the maps of sides 1 to 4 of each image, one map after another, each row by row. `label_numbers`: class of each image; row r belongs to the micro-batch r - 4.
All inputs are finite; a program needn't handle non-finite values.
Results may differ from a plain program's by a relative error of at most 0.0151.
Values may be sent and summed in bfloat16 or wider, within the bound.
No kernel may reach another device: no remote copies, remote signals or barrier semaphores. Data moves between devices by JAX's collectives and lax.ppermute only.
A program may use at most 128 MiB of HBM per device.

v0:
```python
import jax
import jax.numpy as jnp
from jax import lax
from jax.sharding import PartitionSpec as P

FOCUS_GROUPS = 30
HEAD_DIM = 64
SIDE = 5
LOG_CAP = 4.605170185988092


def shifted(value, axis, steps):
    count = lax.axis_size(axis)
    first, last = (max(0, -steps), min(count, count - steps))
    return lax.ppermute(value, axis, [(source, source + steps) for source in range(first, last)])


def crossing_matrix(target, coarse):
    fine_index = jnp.arange(target, dtype=jnp.float32)
    coarse_index = jnp.arange(coarse, dtype=jnp.float32)
    begins = jnp.maximum(fine_index[:, None] / target, coarse_index[None, :] / coarse)
    finish = jnp.minimum(
        (fine_index[:, None] + 1.0) / target, (coarse_index[None, :] + 1.0) / coarse
    )
    return jnp.maximum(finish - begins, 0.0) * target


def resampler():
    blocks = []
    for coarse in range(1, SIDE):
        crossing = crossing_matrix(SIDE, coarse)
        blocks.append(
            (crossing[:, None, :, None] * crossing[None, :, None, :]).reshape(
                SIDE * SIDE, coarse * coarse
            )
        )
    return jnp.concatenate(blocks, axis=1)


def embed(
    drawn_coarse_codes,
    discrete_prototypes,
    code_raising_operator,
    placement_tier_features,
    resample_table,
):
    looked_up = discrete_prototypes[drawn_coarse_codes]
    mapped = jnp.einsum(
        "tc,nicv->nitv", resample_table, looked_up, precision=lax.Precision.HIGHEST
    ).astype(jnp.bfloat16)
    leading = mapped.shape[:3]
    projected_rows = jnp.dot(
        mapped.reshape(-1, mapped.shape[3]),
        code_raising_operator,
        preferred_element_type=jnp.float32,
    )
    projected_rows = projected_rows.reshape(leading + (code_raising_operator.shape[1],))
    return (projected_rows + placement_tier_features.astype(jnp.float32)).astype(jnp.bfloat16)


def norm_mod(latent_stream, scale_term, offset_term):
    widened = latent_stream.astype(jnp.float32)
    average = jnp.mean(widened, axis=-1, keepdims=True)
    centred = widened - average
    spread = jnp.mean(centred * centred, axis=-1, keepdims=True)
    normed = (
        centred * lax.rsqrt(spread + 1e-06) * (1.0 + scale_term[:, None, :])
        + offset_term[:, None, :]
    )
    return normed.astype(jnp.bfloat16)


def attention(qkv_cols, log_scale, cached_keys, cached_values):
    qkv = lax.all_to_all(qkv_cols, "tp", split_axis=0, concat_axis=3, tiled=True)
    images = qkv.shape[0]
    count = qkv.shape[1]
    widened = qkv.astype(jnp.float32)
    query = widened[:, :, 0].reshape(images, count, FOCUS_GROUPS, HEAD_DIM)
    new_keys = widened[:, :, 1].reshape(images, count, FOCUS_GROUPS, HEAD_DIM)
    new_values = qkv[:, :, 2].reshape(images, count, FOCUS_GROUPS, HEAD_DIM)
    head_mult = jnp.exp(jnp.minimum(log_scale, LOG_CAP))
    query = (
        query
        * lax.rsqrt(jnp.sum(query * query, axis=-1, keepdims=True) + 1e-06)
        * head_mult[:, None]
    )
    new_keys = new_keys * lax.rsqrt(jnp.sum(new_keys * new_keys, axis=-1, keepdims=True) + 1e-06)
    all_keys = jnp.concatenate(
        [cached_keys.astype(jnp.float32).reshape(images, -1, FOCUS_GROUPS, HEAD_DIM), new_keys],
        axis=1,
    )
    all_values = jnp.concatenate(
        [cached_values.reshape(images, -1, FOCUS_GROUPS, HEAD_DIM), new_values], axis=1
    )
    scores = jnp.einsum("iqhd,ikhd->ihqk", query, all_keys, precision=lax.Precision.HIGHEST)
    maximum = jnp.max(scores, axis=-1, keepdims=True)
    weights = jnp.exp(scores - maximum)
    probabilities = (weights / jnp.sum(weights, axis=-1, keepdims=True)).astype(jnp.bfloat16)
    mixed = jnp.einsum(
        "ihqk,ikhd->iqhd", probabilities, all_values, preferred_element_type=jnp.float32
    )
    return mixed.reshape(images, count, FOCUS_GROUPS * HEAD_DIM).astype(jnp.bfloat16)


def project_out(attended, out_matrix):
    return jnp.dot(
        lax.all_gather(attended, "tp", axis=0, tiled=True),
        out_matrix,
        preferred_element_type=jnp.float32,
    )


def pass_on(latent_stream):
    return shifted(latent_stream, "section", 1)


def local(
    awaiting_arrivals,
    label_numbers,
    drawn_coarse_codes,
    discrete_prototypes,
    code_raising_operator,
    placement_tier_features,
    label_feature_rows,
    conditioned_gain_mapping,
    conditioned_shift_addend,
    question_answer_operator,
    mixing_return_operator,
    focus_sharpness_exponents,
    prior_resolution_probes,
    prior_resolution_answers,
):
    sections = lax.axis_size("section")
    section_at = lax.axis_index("section")
    group_index = lax.axis_index("tp")
    moments = prior_resolution_probes.shape[1]
    width = question_answer_operator.shape[1]
    column_width = question_answer_operator.shape[3]
    images = drawn_coarse_codes.shape[1]
    resident_pictures = awaiting_arrivals.shape[1]
    class_rows = lax.dynamic_slice_in_dim(label_numbers, sections - 1 - section_at, moments, 0)
    class_part = jnp.take(label_feature_rows, class_rows, axis=0)
    activated_part = jax.nn.silu(class_part.astype(jnp.float32)).astype(jnp.bfloat16)
    gated_response = lax.all_gather(activated_part, "tp", axis=2, tiled=True)
    flat_active = gated_response.reshape(moments * images, width)
    inner_block = 0
    local_mod = conditioned_gain_mapping[inner_block].reshape(width, 3 * column_width)
    modulated = jnp.dot(flat_active, local_mod, preferred_element_type=jnp.float32)
    mod_list = [
        modulated.reshape(moments, images, 3, column_width) + conditioned_shift_addend[inner_block]
    ]
    mod_cols = jnp.stack(mod_list)
    resample_table = resampler()
    emitted = []
    mod_rows = lax.all_to_all(mod_cols, "tp", split_axis=2, concat_axis=4, tiled=True)
    own_tokens = lax.dynamic_slice_in_dim(
        drawn_coarse_codes, group_index * resident_pictures, resident_pictures, 1
    )
    entering = embed(
        own_tokens,
        discrete_prototypes,
        code_raising_operator,
        placement_tier_features,
        resample_table,
    )
    passed_along_activation = awaiting_arrivals[0]
    for clock_tick in range(moments):
        latent_stream = passed_along_activation
        inner_block = 0
        modulation = mod_rows[inner_block, clock_tick]
        normed = norm_mod(latent_stream, modulation[:, 1], modulation[:, 2])
        local_qkv = question_answer_operator[inner_block].reshape(width, 3 * column_width)

        def body_product(portion, offset, local_qkv=local_qkv):
            return jnp.dot(portion, local_qkv, preferred_element_type=jnp.float32).astype(
                jnp.bfloat16
            )

        qkv_cols = body_product(lax.all_gather(normed, "tp", axis=0, tiled=True), jnp.int32(0))
        qkv_cols = qkv_cols.reshape(qkv_cols.shape[0], qkv_cols.shape[1], 3, column_width)
        attended = attention(
            qkv_cols,
            focus_sharpness_exponents[inner_block],
            prior_resolution_probes[inner_block, clock_tick],
            prior_resolution_answers[inner_block, clock_tick],
        )
        projected_cols = project_out(attended, mixing_return_operator[inner_block]).astype(
            jnp.bfloat16
        )
        projected = lax.all_to_all(projected_cols, "tp", split_axis=0, concat_axis=2, tiled=True)
        latent_stream = (
            latent_stream.astype(jnp.float32)
            + modulation[:, 0][:, None, :] * projected.astype(jnp.float32)
        ).astype(jnp.bfloat16)
        emitted.append(latent_stream)
        if clock_tick + 1 < moments:
            arrived = pass_on(latent_stream)
            passed_along_activation = jnp.where(section_at == 0, entering[clock_tick], arrived)
    result = jnp.stack(emitted)
    return result[None]


def solution(mesh):
    in_specs = (
        P("section", "tp", None, None),
        P(),
        P(),
        P(),
        P(),
        P(),
        P(None, "tp"),
        P("section", None, None, "tp"),
        P("section", None, "tp"),
        P("section", None, None, "tp"),
        P("section", None, "tp"),
        P("section", None),
        P("section", None, "tp", None, None),
        P("section", None, "tp", None, None),
    )
    out_specs = P("section", None, "tp", None, None)
    return jax.shard_map(local, mesh=mesh, in_specs=in_specs, out_specs=out_specs, check_vma=False)
```

profile of v0, /device:TPU:4, one launch (start us, length us, event | category | flops | bytes accessed | tf_op | source)
XLA Modules:
  0.0 244.2 jit_solution(13599707762112273153)
XLA Ops:
  0.9 1.2 copy.162
  3.0 16.4 %all_gather.15 = bf16[2,8,1920]{1,0,2:T(2,128)(2,1)S(1)} all-gather(bf16[2,8,240]{1,0,2:T(2,128)(2,1)S(1)} %copy.163), channel_id=1, replica_groups=mesh['section'=4,'tp'=8] {'tp'}, dimensions={2}, use_global_device_ids=true | all-gather | bytes 69120 | tf_op jit(solution)/shard_map/all_gather | solution.py:144
  20.1 2.9 %fusion.17 = f32[1,2,8,3,240]{4,2,3,1,0:T(8,128)S(1)} fusion(bf16[1,1920,3,240]{1,3,2,0:T(8,128)(2,1)} %param.21, bf16[2,8,1920,1]{1,0,2,3:T(2,128)(2,1)S(1)} %bitcast.178, f32[3,240]{1,0:T(4,128)S(1)} %bitcast.180), kind=kOutput, calls=%fused_computation.24 | convolution fusion | flops 44248320 | bytes 2875200 | tf_op jit(solution)/shard_map/dot_general | solution.py:148
  23.7 5.1 %all-to-all-start = ((f32[1,2,8,3,240]{4,1,3,0,2:T(2,128)}), f32[1,2,8,3,240]{4,1,3,0,2:T(2,128)S(1)}, u32[]{:S(2)}, u32[]{:S(2)}) async-start(f32[1,2,8,3,240]{4,1,3,0,2:T(2,128)} %copy.165), calls=%async_computation | async-start | bytes 98304 | tf_op jit(solution)/shard_map/all_to_all | solution.py:155
  29.2 1.5 convert_reduce_fusion.1
  32.4 2.8 %slice_reduce_fusion = (bf16[30,1920]{1,0:T(8,128)(2,1)}, bf16[30,1920]{1,0:T(8,128)(2,1)}) fusion(bf16[1,2,1,30,1920]{4,1,3,2,0:T(2,128)(2,1)} %param.27), kind=kLoop, calls=%fused_computation.77 | loop fusion | bytes 460800 | tf_op jit(solution)/shard_map/slice | solution.py:185
  36.7 17.0 %all_gather.16 = bf16[8,25,1920]{2,1,0:T(8,128)(2,1)S(1)} all-gather(bf16[1,25,1920]{2,1,0:T(8,128)(2,1)S(1)} %fusion.43), channel_id=1, replica_groups=mesh['section'=4,'tp'=8] {'tp'}, dimensions={0}, use_global_device_ids=true | all-gather | bytes 864000 | tf_op jit(solution)/shard_map/all_gather | solution.py:179
  53.6 1.8 convolution_convert_fusion.1
  55.4 1.7 reshape.1148
  58.0 5.2 %all-to-all-start.1 = ((bf16[8,25,3,240]{3,1,2,0:T(8,128)(2,1)}), bf16[8,25,3,240]{3,1,2,0:T(8,128)(2,1)}, u32[]{:S(2)}, u32[]{:S(2)}) async-start(bf16[8,25,3,240]{3,1,2,0:T(8,128)(2,1)} %copy.169), calls=%async_computation.1 | async-start | bytes 786432 | tf_op jit(solution)/shard_map/all_to_all | solution.py:74
  64.0 1.1 copy.175
  65.1 1.1 reshape_squeeze.32
  67.0 3.0 %copy.180 = f32[4096,32]{1,0:T(8,128)} copy(f32[4096,32]{0,1:T(8,128)} %param.17) | data formatting | bytes 1048576 | tf_op args[3]
  73.9 2.8 %gather_fusion.1 = f32[30,32]{1,0:T(8,128)} fusion(f32[4096,32]{1,0:T(8,128)} %copy.180, s32[1024]{0:T(1024)S(1)} %pad_clamp_fusion), kind=kCustom, calls=%fused_computation.1 | custom fusion | bytes 7800 | tf_op jit(solution)/shard_map/gather | solution.py:47
  76.7 1.2 copy.170
  78.4 1.0 fusion.72
  80.2 1.1 reshape_squeeze.36
  82.2 1.4 copy.173
  83.6 1.8 copy_multiply_fusion.1
  85.3 1.1 reshape_squeeze.35
  86.5 1.7 slice_multiply_fusion.1
  88.1 1.9 mul.390
  90.0 1.2 reduce_sum.92
  91.4 2.8 %fusion.24 = f32[30,25,55]{2,1,0:T(8,128)S(1)} fusion(f32[1,25,30,64]{3,1,2,0:T(8,128)} %copy_multiply_fusion.1, f32[1,30,30,64]{3,1,2,0:T(8,128)} %copy.175, f32[25,30,64]{2,1,0:T(8,128)S(1)} %multiply_multiply_fusion.1), kind=kOutput, calls=%fused_computation.31 | convolution fusion | flops 31785600 | bytes 779400 | tf_op jit(solution)/shard_map/iqhd,ikhd->ihqk/dot_general | solution.py:95
  95.5 1.7 copy.172
  97.2 3.5 %fusion.12 = bf16[1,25,30,64]{3,1,2,0:T(8,128)(2,1)} fusion(bf16[1,25,30,64]{3,1,2,0:T(8,128)(2,1)} %copy.172, bf16[1,30,30,64]{3,1,2,0:T(8,128)(2,1)} %copy.171, f32[30,25]{1,0:T(8,128)S(1)} %fusion.73, f32[30,25,55]{2,1,0:T(8,128)S(1)} %fusion.24), kind=kOutput, calls=%fused_computation.19 | convolution fusion | flops 5874954 | bytes 475200 | tf_op jit(solution)/shard_map/ihqk,ikhd->iqhd/dot_general | solution.py:99
  100.7 1.1 copy.177
  102.0 17.0 %all_gather.17 = bf16[8,25,1920]{2,1,0:T(8,128)(2,1)S(1)} all-gather(bf16[1,25,1920]{2,1,0:T(8,128)(2,1)S(1)} %convert_element_type.264), channel_id=1, replica_groups=mesh['section'=4,'tp'=8] {'tp'}, dimensions={0}, use_global_device_ids=true | all-gather | bytes 864000 | tf_op jit(solution)/shard_map/all_gather | solution.py:107
  119.0 2.3 convolution_convert_fusion.5
  121.2 5.2 %all-to-all-start.2 = ((bf16[8,25,240]{2,1,0:T(8,128)(2,1)}), bf16[8,25,240]{2,1,0:T(8,128)(2,1)S(1)}, u32[]{:S(2)}, u32[]{:S(2)}) async-start(bf16[8,25,240]{2,1,0:T(8,128)(2,1)} %convolution_convert_fusion.5), calls=%async_computation.2 | async-start | bytes 262144 | tf_op jit(solution)/shard_map/all_to_all | solution.py:190
  126.7 6.5 %all-to-all-done.2 = bf16[8,25,240]{2,1,0:T(8,128)(2,1)S(1)} async-done(((bf16[8,25,240]{2,1,0:T(8,128)(2,1)}), bf16[8,25,240]{2,1,0:T(8,128)(2,1)S(1)}, u32[]{:S(2)}, u32[]{:S(2)}) %all-to-all-start.2) | async-done | bytes 96032 | tf_op jit(solution)/shard_map/all_to_all | solution.py:190
  133.6 3.4 %collective-permute-start = (bf16[1,25,1920]{2,1,0:T(8,128)(2,1)S(1)}, bf16[1,25,1920]{2,1,0:T(8,128)(2,1)S(1)}, u32[]{:S(2)}, u32[]{:S(2)}) collective-permute-start(bf16[1,25,1920]{2,1,0:T(8,128)(2,1)S(1)} %fusion.44), channel_id=1, source_target_pairs={{0,8},{8,16},{16,24},{1,9},{9,17},{17,25},{2,10},{10,18},{18,26},{... | collective-permute-start | bytes 288008 | tf_op jit(solution)/shard_map/ppermute | solution.py:15
  137.6 3.6 %collective-permute-done = bf16[1,25,1920]{2,1,0:T(8,128)(2,1)S(1)} collective-permute-done((bf16[1,25,1920]{2,1,0:T(8,128)(2,1)S(1)}, bf16[1,25,1920]{2,1,0:T(8,128)(2,1)S(1)}, u32[]{:S(2)}, u32[]{:S(2)}) %collective-permute-start) | collective-permute-done | bytes 96032 | tf_op jit(solution)/shard_map/ppermute | solution.py:15
  141.2 1.3 fusion.74
  142.9 16.3 %all_gather.18 = bf16[8,25,1920]{2,1,0:T(8,128)(2,1)S(1)} all-gather(bf16[1,25,1920]{2,1,0:T(8,128)(2,1)S(1)} %add_convert_fusion.1), channel_id=1, replica_groups=mesh['section'=4,'tp'=8] {'tp'}, dimensions={0}, use_global_device_ids=true | all-gather | bytes 864000 | tf_op jit(solution)/shard_map/all_gather | solution.py:179
  159.2 1.8 convolution_convert_fusion
  161.0 2.4 reshape.1151
  163.4 1.8 copy.187
  165.2 4.3 %all-to-all-start.3 = ((bf16[8,25,3,240]{3,1,2,0:T(8,128)(2,1)}), bf16[8,25,3,240]{3,1,2,0:T(8,128)(2,1)}, u32[]{:S(2)}, u32[]{:S(2)}) async-start(bf16[8,25,3,240]{3,1,2,0:T(8,128)(2,1)} %copy.187), calls=%async_computation.3 | async-start | bytes 786432 | tf_op jit(solution)/shard_map/all_to_all | solution.py:74
  169.5 2.0 reshape.1119
  171.5 2.1 copy.193
  173.6 1.0 reshape_squeeze.37
  174.5 1.7 copy.189
  177.1 4.7 %all-to-all-done.3 = bf16[8,25,3,240]{3,1,2,0:T(8,128)(2,1)} async-done(((bf16[8,25,3,240]{3,1,2,0:T(8,128)(2,1)}), bf16[8,25,3,240]{3,1,2,0:T(8,128)(2,1)}, u32[]{:S(2)}, u32[]{:S(2)}) %all-to-all-start.3) | async-done | bytes 288032 | tf_op jit(solution)/shard_map/all_to_all | solution.py:74
  181.8 1.9 copy.188
  183.7 1.4 all_to_all.65
  186.8 1.9 mul.431
  188.7 1.2 reduce_sum.97
  189.9 1.9 reshape_squeeze.39
  191.8 1.9 reshape_squeeze.40
  193.7 1.2 multiply_reduce_fusion
  196.4 1.3 copy_multiply_fusion
  197.6 1.2 multiply_multiply_fusion
  198.8 2.7 %fusion.27 = f32[30,25,55]{2,1,0:T(8,128)S(1)} fusion(f32[1,25,30,64]{3,1,2,0:T(8,128)S(1)} %copy_multiply_fusion, f32[1,30,30,64]{3,1,2,0:T(8,128)} %copy.193, f32[25,30,64]{2,1,0:T(8,128)S(1)} %multiply_multiply_fusion), kind=kOutput, calls=%fused_computation.35 | convolution fusion | flops 31785600 | bytes 779400 | tf_op jit(solution)/shard_map/iqhd,ikhd->ihqk/dot_general | solution.py:95
  203.6 3.8 %fusion.13 = bf16[1,25,30,64]{3,1,2,0:T(8,128)(2,1)} fusion(bf16[1,25,30,64]{3,1,2,0:T(8,128)(2,1)} %copy.190, bf16[1,30,30,64]{3,1,2,0:T(8,128)(2,1)} %copy.189, f32[30,25]{1,0:T(8,128)S(1)} %fusion.75, f32[30,25,55]{2,1,0:T(8,128)} %copy-done.5), kind=kOutput, calls=%fused_computation.20 | convolution fusion | flops 5874954 | bytes 475200 | tf_op jit(solution)/shard_map/ihqk,ikhd->iqhd/dot_general | solution.py:99
  207.4 1.7 copy.195
  209.2 1.1 convert_element_type.289
  210.3 16.2 %all_gather.19 = bf16[8,25,1920]{2,1,0:T(8,128)(2,1)S(1)} all-gather(bf16[1,25,1920]{2,1,0:T(8,128)(2,1)S(1)} %convert_element_type.289), channel_id=1, replica_groups=mesh['section'=4,'tp'=8] {'tp'}, dimensions={0}, use_global_device_ids=true | all-gather | bytes 864000 | tf_op jit(solution)/shard_map/all_gather | solution.py:107
  226.5 2.3 convolution_convert_fusion.4
  228.8 4.0 %all-to-all-start.4 = ((bf16[8,25,240]{2,1,0:T(8,128)(2,1)}), bf16[8,25,240]{2,1,0:T(8,128)(2,1)}, u32[]{:S(2)}, u32[]{:S(2)}) async-start(bf16[8,25,240]{2,1,0:T(8,128)(2,1)} %convolution_convert_fusion.4), calls=%async_computation.4 | async-start | bytes 262144 | tf_op jit(solution)/shard_map/all_to_all | solution.py:190
  233.5 6.1 %all-to-all-done.4 = bf16[8,25,240]{2,1,0:T(8,128)(2,1)} async-done(((bf16[8,25,240]{2,1,0:T(8,128)(2,1)}), bf16[8,25,240]{2,1,0:T(8,128)(2,1)}, u32[]{:S(2)}, u32[]{:S(2)}) %all-to-all-start.4) | async-done | bytes 96032 | tf_op jit(solution)/shard_map/all_to_all | solution.py:190
  239.6 0.9 convert_bitcast_fusion.1
  241.3 1.1 reshape.1152
  242.4 0.9 maximum_bitcast_fusion.8
  (126 shorter events, 26.8 us)
Async XLA Ops:
  0.0 53.6 %copy-start = (bf16[1,1920,3,240]{1,3,2,0:T(8,128)(2,1)S(1)}, bf16[1,1920,3,240]{1,3,2,0:T(8,128)(2,1)}, u32[]{:S(2)}) copy-start(bf16[1,1920,3,240]{1,3,2,0:T(8,128)(2,1)} %param.23) | copy-start | bytes 8294404
  2.2 26.7 %copy-start.3 = (bf16[1,1,25,1920]{3,2,1,0:T(8,128)(2,1)S(1)}, bf16[1,1,25,1920]{3,2,1,0:T(8,128)(2,1)}, u32[]{:S(2)}) copy-start(bf16[1,1,25,1920]{3,2,1,0:T(8,128)(2,1)} %param.14) | copy-start | bytes 288004
  2.8 26.5 %copy-start.7 = (bf16[1,2,1,30,1920]{4,1,3,2,0:T(2,128)(2,1)S(1)}, bf16[1,2,1,30,1920]{4,1,3,2,0:T(2,128)(2,1)}, u32[]{:S(2)}) copy-start(bf16[1,2,1,30,1920]{4,1,3,2,0:T(2,128)(2,1)} %param.26) | copy-start | bytes 691204
  23.7 11.5 %all-to-all-start = ((f32[1,2,8,3,240]{4,1,3,0,2:T(2,128)}), f32[1,2,8,3,240]{4,1,3,0,2:T(2,128)S(1)}, u32[]{:S(2)}, u32[]{:S(2)}) async-start(f32[1,2,8,3,240]{4,1,3,0,2:T(2,128)} %copy.165), calls=%async_computation | async-start | bytes 98304 | tf_op jit(solution)/shard_map/all_to_all | solution.py:155
  58.0 18.7 %all-to-all-start.1 = ((bf16[8,25,3,240]{3,1,2,0:T(8,128)(2,1)}), bf16[8,25,3,240]{3,1,2,0:T(8,128)(2,1)}, u32[]{:S(2)}, u32[]{:S(2)}) async-start(bf16[8,25,3,240]{3,1,2,0:T(8,128)(2,1)} %copy.169), calls=%async_computation.1 | async-start | bytes 786432 | tf_op jit(solution)/shard_map/all_to_all | solution.py:74
  64.0 6.7 %copy-start.9 = (f32[5,5,3,3]{1,0,3,2:T(8,128)S(1)}, f32[5,5,3,3]{1,0,3,2:T(8,128)}, u32[]{:S(2)}) copy-start(f32[5,5,3,3]{1,0,3,2:T(8,128)} %broadcast_multiply_fusion.1) | copy-start | bytes 2704
  64.0 7.5 %copy-start.12 = (f32[5,5,2,2]{1,0,3,2:T(8,128)S(1)}, f32[5,5,2,2]{1,0,3,2:T(8,128)}, u32[]{:S(2)}) copy-start(f32[5,5,2,2]{1,0,3,2:T(8,128)} %broadcast_multiply_fusion.2) | copy-start | bytes 1204
  64.0 8.3 %copy-start.19 = (f32[5]{0:T(128)S(1)}, f32[5]{0:T(128)}, u32[]{:S(2)}) copy-start(f32[5]{0:T(128)} %maximum_multiply_fusion.3) | copy-start | bytes 64
  64.0 12.7 %copy-start.20 = (f32[1,30]{1,0:T(1,128)S(1)}, f32[1,30]{1,0:T(1,128)}, u32[]{:S(2)}) copy-start(f32[1,30]{1,0:T(1,128)} %param.25) | copy-start | bytes 364
  78.4 9.8 %copy-start.1 = (bf16[1,25,3,1920]{3,1,2,0:T(8,128)(2,1)}, bf16[1,25,3,1920]{3,1,2,0:T(8,128)(2,1)S(1)}, u32[]{:S(2)}) copy-start(bf16[1,25,3,1920]{3,1,2,0:T(8,128)(2,1)S(1)} %all_to_all.60) | copy-start | bytes 864004
  90.0 4.6 %slice-start = ((bf16[1,25,3,1920]{3,1,2,0:T(8,128)(2,1)}), bf16[1,25,1,1920]{3,1,2,0:T(8,128)(2,1)S(1)}, s32[]{:S(2)}) async-start(bf16[1,25,3,1920]{3,1,2,0:T(8,128)(2,1)} %copy-done.1), calls=%async_computation.5 | async-start | bytes 245760 | tf_op jit(solution)/shard_map/slice | solution.py:80
  100.6 25.8 %copy-start.13 = (f32[30,32]{1,0:T(8,128)S(1)}, f32[30,32]{1,0:T(8,128)}, u32[]{:S(2)}) copy-start(f32[30,32]{1,0:T(8,128)} %gather_fusion.1) | copy-start | bytes 11524
  100.6 25.8 %copy-start.14 = (f32[25,9]{1,0:T(8,128)S(1)}, f32[25,9]{1,0:T(8,128)}, u32[]{:S(2)}) copy-start(f32[25,9]{1,0:T(8,128)} %copy.183) | copy-start | bytes 2704
  100.6 25.8 %copy-start.15 = (f32[25,4]{1,0:T(8,128)S(1)}, f32[25,4]{1,0:T(8,128)}, u32[]{:S(2)}) copy-start(f32[25,4]{1,0:T(8,128)} %copy.182) | copy-start | bytes 1204
  100.6 25.8 %copy-start.16 = (f32[25,1]{1,0:T(8,128)S(1)}, f32[25,1]{1,0:T(8,128)}, u32[]{:S(2)}) copy-start(f32[25,1]{1,0:T(8,128)} %copy.181) | copy-start | bytes 304
  100.6 25.8 %copy-start.17 = (f32[25,16]{1,0:T(8,128)S(1)}, f32[25,16]{1,0:T(8,128)}, u32[]{:S(2)}) copy-start(f32[25,16]{1,0:T(8,128)} %mul.419) | copy-start | bytes 4804
  100.7 32.9 %copy-start.4 = (bf16[1,1,25,1920]{3,2,1,0:T(8,128)(2,1)S(1)}, bf16[1,1,25,1920]{3,2,1,0:T(8,128)(2,1)}, u32[]{:S(2)}) copy-start(bf16[1,1,25,1920]{3,2,1,0:T(8,128)(2,1)} %param.14) | copy-start | bytes 288004
  100.7 32.9 %copy-start.11 = (f32[1920]{0:T(1024)S(1)}, f32[1920]{0:T(1024)}, u32[]{:S(2)}) copy-start(f32[1920]{0:T(1024)} %get-tuple-element.12) | copy-start | bytes 23044
  101.8 35.2 %copy-start.10 = (f32[1,3,1920]{2,0,1:T(1,128)S(1)}, f32[1,3,1920]{2,0,1:T(1,128)}, u32[]{:S(2)}) copy-start(f32[1,3,1920]{2,0,1:T(1,128)} %get-tuple-element.21) | copy-start | bytes 69124
  121.2 11.9 %all-to-all-start.2 = ((bf16[8,25,240]{2,1,0:T(8,128)(2,1)}), bf16[8,25,240]{2,1,0:T(8,128)(2,1)S(1)}, u32[]{:S(2)}, u32[]{:S(2)}) async-start(bf16[8,25,240]{2,1,0:T(8,128)(2,1)} %convolution_convert_fusion.5), calls=%async_computation.2 | async-start | bytes 262144 | tf_op jit(solution)/shard_map/all_to_all | solution.py:190
  133.6 7.7 %collective-permute-start = (bf16[1,25,1920]{2,1,0:T(8,128)(2,1)S(1)}, bf16[1,25,1920]{2,1,0:T(8,128)(2,1)S(1)}, u32[]{:S(2)}, u32[]{:S(2)}) collective-permute-start(bf16[1,25,1920]{2,1,0:T(8,128)(2,1)S(1)} %fusion.44), channel_id=1, source_target_pairs={{0,8},{8,16},{16,24},{1,9},{9,17},{17,25},{2,10},{10,18},{18,26},{... | collective-permute-start | bytes 288008 | tf_op jit(solution)/shard_map/ppermute | solution.py:15
  161.0 12.6 %copy-start.8 = (bf16[30,1920]{1,0:T(8,128)(2,1)S(1)}, bf16[30,1920]{1,0:T(8,128)(2,1)}, u32[]{:S(2)}) copy-start(bf16[30,1920]{1,0:T(8,128)(2,1)} %get-tuple-element.7) | copy-start | bytes 345604
  165.2 16.6 %all-to-all-start.3 = ((bf16[8,25,3,240]{3,1,2,0:T(8,128)(2,1)}), bf16[8,25,3,240]{3,1,2,0:T(8,128)(2,1)}, u32[]{:S(2)}, u32[]{:S(2)}) async-start(bf16[8,25,3,240]{3,1,2,0:T(8,128)(2,1)} %copy.187), calls=%async_computation.3 | async-start | bytes 786432 | tf_op jit(solution)/shard_map/all_to_all | solution.py:74
  185.2 9.7 %copy-start.2 = (bf16[1,25,3,1920]{3,1,2,0:T(8,128)(2,1)}, bf16[1,25,3,1920]{3,1,2,0:T(8,128)(2,1)S(1)}, u32[]{:S(2)}) copy-start(bf16[1,25,3,1920]{3,1,2,0:T(8,128)(2,1)S(1)} %all_to_all.65) | copy-start | bytes 864004
  195.5 7.1 %slice-start.1 = ((bf16[1,25,3,1920]{3,1,2,0:T(8,128)(2,1)}), bf16[1,25,1,1920]{3,1,2,0:T(8,128)(2,1)S(1)}, s32[]{:S(2)}) async-start(bf16[1,25,3,1920]{3,1,2,0:T(8,128)(2,1)} %copy-done.2), calls=%async_computation.6 | async-start | bytes 245760 | tf_op jit(solution)/shard_map/slice | solution.py:80
  201.5 0.8 copy-start.5
  207.4 25.4 %copy-start.6 = (f32[1,1,25,1920]{3,2,1,0:T(8,128)S(1)}, f32[1,1,25,1920]{3,2,1,0:T(8,128)}, u32[]{:S(2)}) copy-start(f32[1,1,25,1920]{3,2,1,0:T(8,128)} %reshape.1149) | copy-start | bytes 576004
  209.2 33.2 %copy-start.18 = (f32[1920]{0:T(1024)S(1)}, f32[1920]{0:T(1024)}, u32[]{:S(2)}) copy-start(f32[1920]{0:T(1024)} %get-tuple-element.9) | copy-start | bytes 23044
  228.8 10.8 %all-to-all-start.4 = ((bf16[8,25,240]{2,1,0:T(8,128)(2,1)}), bf16[8,25,240]{2,1,0:T(8,128)(2,1)}, u32[]{:S(2)}, u32[]{:S(2)}) async-start(bf16[8,25,240]{2,1,0:T(8,128)(2,1)} %convolution_convert_fusion.4), calls=%async_computation.4 | async-start | bytes 262144 | tf_op jit(solution)/shard_map/all_to_all | solution.py:190
where the time goes:
time: 246 us; the launch traced here: 244 us
  blocking collectives  82.9 us (34%)
  local copies, waits for them, and re-layouts  63.8 us (26%)
  starting transfers between devices  27.2 us (11%)
  matrix products  25.3 us (10%)
  other arithmetic  23.5 us (10%)
  waiting for transfers between devices  20.9 us (8%)
    all_gather x2, blocking collectives, local(): lax.all_gather(normed, 'tp', axis=0, tiled=True)  33.3 us
    all_gather x2, blocking collectives, project_out(): lax.all_gather(attended, 'tp', axis=0, tiled=True)  33.2 us
    all_gather x1, blocking collectives, local(): gated_response = lax.all_gather(activated_part, 'tp', axis=2, tiled=True)  16.4 us
    all_to_all x2, waiting for transfers between devices, local(): lax.all_to_all(projected_cols, 'tp', split_axis=0, concat_axis=2, tiled=T...  12.5 us
    all_to_all x2, starting transfers between devices, attention(): lax.all_to_all(qkv_cols, 'tp', split_axis=0, concat_axis=3, tiled=True)  9.52 us
    all_to_all x2, starting transfers between devices, local(): lax.all_to_all(projected_cols, 'tp', split_axis=0, concat_axis=2, tiled=T...  9.2 us
    dot_general x2, matrix products, attention(): jnp.einsum('ihqk,ikhd->iqhd', probabilities, all_values, preferred_elemen...  7.32 us
    reshape x4, local copies, waits for them, and re-layouts, local(): qkv_cols.reshape(qkv_cols.shape[0], qkv_cols.shape[1], 3, column_width)  6.8 us
  transfers between devices with their start and end apart: 6, of which 4 were waited for; matrix products, arithmetic and copies ran while one was open for 12% of the time, Pallas kernels for 0%

commit v1 on v0

--- a/solution.py
+++ b/solution.py
@@ -104,7 +104,9 @@
 
 def project_out(attended, out_matrix):
     return jnp.dot(
-        lax.all_gather(attended, "tp", axis=0, tiled=True),
+        jnp.concatenate(
+            lax.all_to_all(jnp.stack([attended] * lax.axis_size("tp")), "tp", 0, 0), axis=0
+        ),
         out_matrix,
         preferred_element_type=jnp.float32,
     )

time: 246 us -> 275 us (1.12)
  waiting for transfers between devices: 20.9 us -> 79.1 us
  blocking collectives: 82.9 us -> 49.7 us
  starting transfers between devices: 27.2 us -> 34 us
  local copies, waits for them, and re-layouts: 63.8 us -> 59.7 us
    all_to_all x0 -> x2, waiting for transfers between devices: none -> 45.5 us  [project_out(): lax.all_to_all(jnp.stack([attended] * lax.axis_size('tp')), 'tp', 0, 0)]
    all_gather x2 -> x0, blocking collectives: 33.2 us -> none  [project_out(): lax.all_gather(attended, 'tp', axis=0, tiled=True)]
    all_to_all x2, waiting for transfers between devices: 4.72 us -> 18.4 us  [attention(): lax.all_to_all(qkv_cols, 'tp', split_axis=0, concat_axis=3, tiled=True)]
    all_to_all x0 -> x2, starting transfers between devices: none -> 8.6 us  [project_out(): lax.all_to_all(jnp.stack([attended] * lax.axis_size('tp')), 'tp', 0, 0)]
    unnamed x45 -> x49, local copies, waits for them, and re-layouts: 5.77 us -> 5.82 us
  transfers between devices with their start and end apart: 6 -> 8, of which waited for: 4 -> 7; matrix products, arithmetic and copies ran while one was open for 12% -> 9% of each run, Pallas kernels for 0% -> 0%
where the time goes in v1:
time: 275 us; the launch traced here: 273 us
  waiting for transfers between devices  79.1 us (29%)
  local copies, waits for them, and re-layouts  59.7 us (22%)
  blocking collectives  49.7 us (18%)
  starting transfers between devices  34 us (12%)
  matrix products  26.6 us (10%)
  other arithmetic  23.1 us (8%)
    all_to_all x2, waiting for transfers between devices, project_out(): lax.all_to_all(jnp.stack([attended] * lax.axis_size('tp')), 'tp', 0, 0)  45.5 us
    all_gather x2, blocking collectives, local(): lax.all_gather(normed, 'tp', axis=0, tiled=True)  33.3 us
    all_to_all x2, waiting for transfers between devices, attention(): lax.all_to_all(qkv_cols, 'tp', split_axis=0, concat_axis=3, tiled=True)  18.4 us
    all_gather x1, blocking collectives, local(): gated_response = lax.all_gather(activated_part, 'tp', axis=2, tiled=True)  16.4 us
    all_to_all x2, waiting for transfers between devices, local(): lax.all_to_all(projected_cols, 'tp', split_axis=0, concat_axis=2, tiled=T...  11 us
    all_to_all x2, starting transfers between devices, attention(): lax.all_to_all(qkv_cols, 'tp', split_axis=0, concat_axis=3, tiled=True)  9.52 us
    all_to_all x2, starting transfers between devices, project_out(): lax.all_to_all(jnp.stack([attended] * lax.axis_size('tp')), 'tp', 0, 0)  8.6 us
    all_to_all x2, starting transfers between devices, local(): lax.all_to_all(projected_cols, 'tp', split_axis=0, concat_axis=2, tiled=T...  7.37 us
  transfers between devices with their start and end apart: 8, of which 7 were waited for; matrix products, arithmetic and copies ran while one was open for 9% of the time, Pallas kernels for 0%

profile of v1, /device:TPU:4, one launch (start us, length us, event | category | flops | bytes accessed | tf_op | source)
XLA Modules:
  0.0 272.7 jit_solution(7386561358345846522)
XLA Ops:
  0.9 1.2 copy.162
  3.0 16.4 %all_gather.9 = bf16[2,8,1920]{1,0,2:T(2,128)(2,1)S(1)} all-gather(bf16[2,8,240]{1,0,2:T(2,128)(2,1)S(1)} %copy.163), channel_id=1, replica_groups=mesh['section'=4,'tp'=8] {'tp'}, dimensions={2}, use_global_device_ids=true | all-gather | bytes 69120 | tf_op jit(solution)/shard_map/all_gather | solution.py:146
  20.2 2.9 %fusion.17 = f32[1,2,8,3,240]{4,2,3,1,0:T(8,128)S(1)} fusion(bf16[1,1920,3,240]{1,3,2,0:T(8,128)(2,1)} %param.21, bf16[2,8,1920,1]{1,0,2,3:T(2,128)(2,1)S(1)} %bitcast.182, f32[3,240]{1,0:T(4,128)S(1)} %bitcast.185), kind=kOutput, calls=%fused_computation.24 | convolution fusion | flops 44248320 | bytes 2875200 | tf_op jit(solution)/shard_map/dot_general | solution.py:150
  23.7 5.1 %all-to-all-start = ((f32[1,2,8,3,240]{4,1,3,0,2:T(2,128)}), f32[1,2,8,3,240]{4,1,3,0,2:T(2,128)S(1)}, u32[]{:S(2)}, u32[]{:S(2)}) async-start(f32[1,2,8,3,240]{4,1,3,0,2:T(2,128)} %copy.165), calls=%async_computation | async-start | bytes 98304 | tf_op jit(solution)/shard_map/all_to_all | solution.py:157
  29.8 1.9 convert_reduce_fusion.1
  31.8 1.6 slice_reduce_fusion
  33.4 1.2 reshape.1122
  34.6 1.1 copy.175
  36.7 3.0 %copy.180 = f32[4096,32]{1,0:T(8,128)} copy(f32[4096,32]{0,1:T(8,128)} %param.17) | data formatting | bytes 1048576 | tf_op args[3]
  40.7 17.0 %all_gather.10 = bf16[8,25,1920]{2,1,0:T(8,128)(2,1)S(1)} all-gather(bf16[1,25,1920]{2,1,0:T(8,128)(2,1)S(1)} %fusion.45), channel_id=1, replica_groups=mesh['section'=4,'tp'=8] {'tp'}, dimensions={0}, use_global_device_ids=true | all-gather | bytes 864000 | tf_op jit(solution)/shard_map/all_gather | solution.py:181
  57.6 1.8 convolution_convert_fusion.1
  59.4 1.7 reshape.1154
  62.0 5.2 %all-to-all-start.1 = ((bf16[8,25,3,240]{3,1,2,0:T(8,128)(2,1)}), bf16[8,25,3,240]{3,1,2,0:T(8,128)(2,1)S(1)}, u32[]{:S(2)}, u32[]{:S(2)}) async-start(bf16[8,25,3,240]{3,1,2,0:T(8,128)(2,1)} %copy.169), calls=%async_computation.1 | async-start | bytes 786432 | tf_op jit(solution)/shard_map/all_to_all | solution.py:74
  68.5 11.2 %all-to-all-done.1 = bf16[8,25,3,240]{3,1,2,0:T(8,128)(2,1)S(1)} async-done(((bf16[8,25,3,240]{3,1,2,0:T(8,128)(2,1)}), bf16[8,25,3,240]{3,1,2,0:T(8,128)(2,1)S(1)}, u32[]{:S(2)}, u32[]{:S(2)}) %all-to-all-start.1) | async-done | bytes 288032 | tf_op jit(solution)/shard_map/all_to_all | solution.py:74
  82.2 1.1 reshape_squeeze.36
  84.2 1.4 copy.173
  85.6 1.8 copy_multiply_fusion.1
  87.3 1.1 reshape_squeeze.35
  88.5 1.7 slice_multiply_fusion.1
  90.1 1.9 mul.390
  92.0 1.2 reduce_sum.92
  93.5 2.8 %fusion.26 = f32[30,25,55]{2,1,0:T(8,128)S(1)} fusion(f32[1,25,30,64]{3,1,2,0:T(8,128)} %copy_multiply_fusion.1, f32[1,30,30,64]{3,1,2,0:T(8,128)} %copy.175, f32[25,30,64]{2,1,0:T(8,128)S(1)} %multiply_multiply_fusion.1), kind=kOutput, calls=%fused_computation.33 | convolution fusion | flops 31785600 | bytes 779400 | tf_op jit(solution)/shard_map/iqhd,ikhd->ihqk/dot_general | solution.py:95
  97.5 1.7 copy.172
  99.2 3.5 %fusion.12 = bf16[1,25,30,64]{3,1,2,0:T(8,128)(2,1)} fusion(bf16[1,25,30,64]{3,1,2,0:T(8,128)(2,1)} %copy.172, bf16[1,30,30,64]{3,1,2,0:T(8,128)(2,1)} %copy.171, f32[30,25]{1,0:T(8,128)S(1)} %fusion.75, f32[30,25,55]{2,1,0:T(8,128)S(1)} %fusion.26), kind=kOutput, calls=%fused_computation.19 | convolution fusion | flops 5874954 | bytes 475200 | tf_op jit(solution)/shard_map/ihqk,ikhd->iqhd/dot_general | solution.py:99
  102.7 1.0 copy.177
  103.9 1.0 stack.11
  105.0 4.4 %all-to-all-start.2 = ((bf16[8,1,25,1920]{3,2,1,0:T(8,128)(2,1)}), bf16[8,1,25,1920]{3,2,1,0:T(8,128)(2,1)}, u32[]{:S(2)}, u32[]{:S(2)}) async-start(bf16[8,1,25,1920]{3,2,1,0:T(8,128)(2,1)} %stack.11), calls=%async_computation.2 | async-start | bytes 1966080 | tf_op jit(solution)/shard_map/all_to_all | solution.py:108
  111.2 2.2 gather_fusion.1
  113.3 21.2 %all-to-all-done.2 = bf16[8,1,25,1920]{3,2,1,0:T(8,128)(2,1)} async-done(((bf16[8,1,25,1920]{3,2,1,0:T(8,128)(2,1)}), bf16[8,1,25,1920]{3,2,1,0:T(8,128)(2,1)}, u32[]{:S(2)}, u32[]{:S(2)}) %all-to-all-start.2) | async-done | bytes 768032 | tf_op jit(solution)/shard_map/all_to_all | solution.py:108
  134.5 2.6 convolution_convert_fusion.5
  137.1 3.4 %all-to-all-start.3 = ((bf16[8,25,240]{2,1,0:T(8,128)(2,1)}), bf16[8,25,240]{2,1,0:T(8,128)(2,1)S(1)}, u32[]{:S(2)}, u32[]{:S(2)}) async-start(bf16[8,25,240]{2,1,0:T(8,128)(2,1)} %convolution_convert_fusion.5), calls=%async_computation.3 | async-start | bytes 262144 | tf_op jit(solution)/shard_map/all_to_all | solution.py:192
  141.3 5.8 %all-to-all-done.3 = bf16[8,25,240]{2,1,0:T(8,128)(2,1)S(1)} async-done(((bf16[8,25,240]{2,1,0:T(8,128)(2,1)}), bf16[8,25,240]{2,1,0:T(8,128)(2,1)S(1)}, u32[]{:S(2)}, u32[]{:S(2)}) %all-to-all-start.3) | async-done | bytes 96032 | tf_op jit(solution)/shard_map/all_to_all | solution.py:192
  147.6 3.4 %collective-permute-start = (bf16[1,25,1920]{2,1,0:T(8,128)(2,1)S(1)}, bf16[1,25,1920]{2,1,0:T(8,128)(2,1)S(1)}, u32[]{:S(2)}, u32[]{:S(2)}) collective-permute-start(bf16[1,25,1920]{2,1,0:T(8,128)(2,1)S(1)} %fusion.46), channel_id=1, source_target_pairs={{0,8},{8,16},{16,24},{1,9},{9,17},{17,25},{2,10},{10,18},{18,26},{... | collective-permute-start | bytes 288008 | tf_op jit(solution)/shard_map/ppermute | solution.py:15
  151.0 4.2 %collective-permute-done = bf16[1,25,1920]{2,1,0:T(8,128)(2,1)S(1)} collective-permute-done((bf16[1,25,1920]{2,1,0:T(8,128)(2,1)S(1)}, bf16[1,25,1920]{2,1,0:T(8,128)(2,1)S(1)}, u32[]{:S(2)}, u32[]{:S(2)}) %collective-permute-start) | collective-permute-done | bytes 96032 | tf_op jit(solution)/shard_map/ppermute | solution.py:15
  155.2 1.3 fusion.76
  156.9 16.3 %all_gather.11 = bf16[8,25,1920]{2,1,0:T(8,128)(2,1)S(1)} all-gather(bf16[1,25,1920]{2,1,0:T(8,128)(2,1)S(1)} %add_convert_fusion.1), channel_id=1, replica_groups=mesh['section'=4,'tp'=8] {'tp'}, dimensions={0}, use_global_device_ids=true | all-gather | bytes 864000 | tf_op jit(solution)/shard_map/all_gather | solution.py:181
  173.2 1.8 convolution_convert_fusion
  175.0 2.4 reshape.1157
  177.4 1.8 copy.187
  179.2 4.3 %all-to-all-start.4 = ((bf16[8,25,3,240]{3,1,2,0:T(8,128)(2,1)}), bf16[8,25,3,240]{3,1,2,0:T(8,128)(2,1)}, u32[]{:S(2)}, u32[]{:S(2)}) async-start(bf16[8,25,3,240]{3,1,2,0:T(8,128)(2,1)} %copy.187), calls=%async_computation.4 | async-start | bytes 786432 | tf_op jit(solution)/shard_map/all_to_all | solution.py:74
  183.6 2.0 reshape.1125
  185.5 2.1 copy.193
  188.6 7.2 %all-to-all-done.4 = bf16[8,25,3,240]{3,1,2,0:T(8,128)(2,1)} async-done(((bf16[8,25,3,240]{3,1,2,0:T(8,128)(2,1)}), bf16[8,25,3,240]{3,1,2,0:T(8,128)(2,1)}, u32[]{:S(2)}, u32[]{:S(2)}) %all-to-all-start.4) | async-done | bytes 288032 | tf_op jit(solution)/shard_map/all_to_all | solution.py:74
  195.9 1.9 copy.188
  197.8 1.4 all_to_all.72
  200.8 1.9 mul.431
  202.7 1.2 reduce_sum.97
  203.9 1.9 reshape_squeeze.39
  205.8 1.9 reshape_squeeze.40
  207.7 1.2 multiply_reduce_fusion
  210.4 1.3 copy_multiply_fusion
  211.7 1.2 multiply_multiply_fusion
  212.8 2.7 fusion.29
  217.6 3.9 %fusion.13 = bf16[1,25,30,64]{3,1,2,0:T(8,128)(2,1)} fusion(bf16[1,25,30,64]{3,1,2,0:T(8,128)(2,1)} %copy.190, bf16[1,30,30,64]{3,1,2,0:T(8,128)(2,1)} %copy.189, f32[30,25]{1,0:T(8,128)S(1)} %fusion.77, f32[30,25,55]{2,1,0:T(8,128)} %copy-done.5), kind=kOutput, calls=%fused_computation.20 | convolution fusion | flops 5874954 | bytes 475200 | tf_op jit(solution)/shard_map/ihqk,ikhd->iqhd/dot_general | solution.py:99
  221.5 1.7 copy.195
  223.2 1.1 convert_element_type.287
  224.3 1.1 stack.12
  225.3 4.2 %all-to-all-start.5 = ((bf16[8,1,25,1920]{3,2,1,0:T(8,128)(2,1)}), bf16[8,1,25,1920]{3,2,1,0:T(8,128)(2,1)}, u32[]{:S(2)}, u32[]{:S(2)}) async-start(bf16[8,1,25,1920]{3,2,1,0:T(8,128)(2,1)} %stack.12), calls=%async_computation.5 | async-start | bytes 1966080 | tf_op jit(solution)/shard_map/all_to_all | solution.py:108
  230.4 24.3 %all-to-all-done.5 = bf16[8,1,25,1920]{3,2,1,0:T(8,128)(2,1)} async-done(((bf16[8,1,25,1920]{3,2,1,0:T(8,128)(2,1)}), bf16[8,1,25,1920]{3,2,1,0:T(8,128)(2,1)}, u32[]{:S(2)}, u32[]{:S(2)}) %all-to-all-start.5) | async-done | bytes 768032 | tf_op jit(solution)/shard_map/all_to_all | solution.py:108
  254.7 2.6 convolution_convert_fusion.4
  257.3 4.0 %all-to-all-start.6 = ((bf16[8,25,240]{2,1,0:T(8,128)(2,1)}), bf16[8,25,240]{2,1,0:T(8,128)(2,1)}, u32[]{:S(2)}, u32[]{:S(2)}) async-start(bf16[8,25,240]{2,1,0:T(8,128)(2,1)} %convolution_convert_fusion.4), calls=%async_computation.6 | async-start | bytes 262144 | tf_op jit(solution)/shard_map/all_to_all | solution.py:192
  261.3 1.6 fusion.47
  263.0 5.1 %all-to-all-done.6 = bf16[8,25,240]{2,1,0:T(8,128)(2,1)} async-done(((bf16[8,25,240]{2,1,0:T(8,128)(2,1)}), bf16[8,25,240]{2,1,0:T(8,128)(2,1)}, u32[]{:S(2)}, u32[]{:S(2)}) %all-to-all-start.6) | async-done | bytes 96032 | tf_op jit(solution)/shard_map/all_to_all | solution.py:192
  269.8 1.1 reshape.1158
  (134 shorter events, 27.1 us)
Async XLA Ops:
  0.0 57.6 %copy-start = (bf16[1,1920,3,240]{1,3,2,0:T(8,128)(2,1)S(1)}, bf16[1,1920,3,240]{1,3,2,0:T(8,128)(2,1)}, u32[]{:S(2)}) copy-start(bf16[1,1920,3,240]{1,3,2,0:T(8,128)(2,1)} %param.23) | copy-start | bytes 8294404
  2.2 26.7 %copy-start.3 = (bf16[1,1,25,1920]{3,2,1,0:T(8,128)(2,1)S(1)}, bf16[1,1,25,1920]{3,2,1,0:T(8,128)(2,1)}, u32[]{:S(2)}) copy-start(bf16[1,1,25,1920]{3,2,1,0:T(8,128)(2,1)} %param.14) | copy-start | bytes 288004
  2.8 27.0 %copy-start.8 = (bf16[1,2,1,30,1920]{4,1,3,2,0:T(2,128)(2,1)S(1)}, bf16[1,2,1,30,1920]{4,1,3,2,0:T(2,128)(2,1)}, u32[]{:S(2)}) copy-start(bf16[1,2,1,30,1920]{4,1,3,2,0:T(2,128)(2,1)} %param.26) | copy-start | bytes 691204
  19.5 12.3 %copy-start.9 = (bf16[1,2,1,30,1920]{4,1,3,2,0:T(2,128)(2,1)S(1)}, bf16[1,2,1,30,1920]{4,1,3,2,0:T(2,128)(2,1)}, u32[]{:S(2)}) copy-start(bf16[1,2,1,30,1920]{4,1,3,2,0:T(2,128)(2,1)} %param.27) | copy-start | bytes 691204
  23.7 16.0 %all-to-all-start = ((f32[1,2,8,3,240]{4,1,3,0,2:T(2,128)}), f32[1,2,8,3,240]{4,1,3,0,2:T(2,128)S(1)}, u32[]{:S(2)}, u32[]{:S(2)}) async-start(f32[1,2,8,3,240]{4,1,3,0,2:T(2,128)} %copy.165), calls=%async_computation | async-start | bytes 98304 | tf_op jit(solution)/shard_map/all_to_all | solution.py:157
  28.9 4.5 %copy-start.13 = (f32[5]{0:T(128)}, f32[5]{0:T(128)S(1)}, u32[]{:S(2)}) copy-start(f32[5]{0:T(128)S(1)} %get-tuple-element.25) | copy-start | bytes 64
  28.9 4.5 %copy-start.15 = (f32[5]{0:T(128)}, f32[5]{0:T(128)S(1)}, u32[]{:S(2)}) copy-start(f32[5]{0:T(128)S(1)} %get-tuple-element.26) | copy-start | bytes 64
  29.1 4.4 %copy-start.17 = (f32[25]{0:T(128)}, f32[25]{0:T(128)S(1)}, u32[]{:S(2)}) copy-start(f32[25]{0:T(128)S(1)} %broadcast_multiply_fusion.4) | copy-start | bytes 304
  35.6 4.9 %copy-start.18 = (f32[25]{0:T(128)S(1)}, f32[25]{0:T(128)}, u32[]{:S(2)}) copy-start(f32[25]{0:T(128)} %copy-done.17) | copy-start | bytes 304
  35.6 4.9 %copy-start.19 = (f32[25]{0:T(128)S(1)}, f32[25]{0:T(128)}, u32[]{:S(2)}) copy-start(f32[25]{0:T(128)} %add_rsqrt_fusion.5) | copy-start | bytes 304
  57.6 10.9 %copy-start.22 = (f32[1,30]{1,0:T(1,128)S(1)}, f32[1,30]{1,0:T(1,128)}, u32[]{:S(2)}) copy-start(f32[1,30]{1,0:T(1,128)} %param.25) | copy-start | bytes 364
  62.0 17.7 %all-to-all-start.1 = ((bf16[8,25,3,240]{3,1,2,0:T(8,128)(2,1)}), bf16[8,25,3,240]{3,1,2,0:T(8,128)(2,1)S(1)}, u32[]{:S(2)}, u32[]{:S(2)}) async-start(bf16[8,25,3,240]{3,1,2,0:T(8,128)(2,1)} %copy.169), calls=%async_computation.1 | async-start | bytes 786432 | tf_op jit(solution)/shard_map/all_to_all | solution.py:74
  80.4 9.8 %copy-start.1 = (bf16[1,25,3,1920]{3,1,2,0:T(8,128)(2,1)}, bf16[1,25,3,1920]{3,1,2,0:T(8,128)(2,1)S(1)}, u32[]{:S(2)}) copy-start(bf16[1,25,3,1920]{3,1,2,0:T(8,128)(2,1)S(1)} %all_to_all.66) | copy-start | bytes 864004
  92.0 4.6 %slice-start = ((bf16[1,25,3,1920]{3,1,2,0:T(8,128)(2,1)}), bf16[1,25,1,1920]{3,1,2,0:T(8,128)(2,1)S(1)}, s32[]{:S(2)}) async-start(bf16[1,25,3,1920]{3,1,2,0:T(8,128)(2,1)} %copy-done.1), calls=%async_computation.7 | async-start | bytes 245760 | tf_op jit(solution)/shard_map/slice | solution.py:80
  99.2 10.1 %copy-start.14 = (f32[5]{0:T(128)S(1)}, f32[5]{0:T(128)}, u32[]{:S(2)}) copy-start(f32[5]{0:T(128)} %copy-done.13) | copy-start | bytes 64
  99.2 10.1 %copy-start.16 = (f32[5]{0:T(128)S(1)}, f32[5]{0:T(128)}, u32[]{:S(2)}) copy-start(f32[5]{0:T(128)} %copy-done.15) | copy-start | bytes 64
  99.2 10.2 %copy-start.20 = (f32[3]{0:T(128)S(1)}, f32[3]{0:T(128)}, u32[]{:S(2)}) copy-start(f32[3]{0:T(128)} %get-tuple-element.29) | copy-start | bytes 40
  102.7 6.7 %copy-start.21 = (f32[3]{0:T(128)S(1)}, f32[3]{0:T(128)}, u32[]{:S(2)}) copy-start(f32[3]{0:T(128)} %get-tuple-element.30) | copy-start | bytes 40
  103.9 36.6 %copy-start.12 = (f32[25,16]{1,0:T(8,128)S(1)}, f32[25,16]{1,0:T(8,128)}, u32[]{:S(2)}) copy-start(f32[25,16]{1,0:T(8,128)} %mul.419) | copy-start | bytes 4804
  105.0 42.5 %copy-start.4 = (bf16[1,1,25,1920]{3,2,1,0:T(8,128)(2,1)S(1)}, bf16[1,1,25,1920]{3,2,1,0:T(8,128)(2,1)}, u32[]{:S(2)}) copy-start(bf16[1,1,25,1920]{3,2,1,0:T(8,128)(2,1)} %param.14) | copy-start | bytes 288004
  105.0 29.5 %all-to-all-start.2 = ((bf16[8,1,25,1920]{3,2,1,0:T(8,128)(2,1)}), bf16[8,1,25,1920]{3,2,1,0:T(8,128)(2,1)}, u32[]{:S(2)}, u32[]{:S(2)}) async-start(bf16[8,1,25,1920]{3,2,1,0:T(8,128)(2,1)} %stack.11), calls=%async_computation.2 | async-start | bytes 1966080 | tf_op jit(solution)/shard_map/all_to_all | solution.py:108
  109.4 41.6 %copy-start.11 = (f32[1,3,1920]{2,0,1:T(1,128)S(1)}, f32[1,3,1920]{2,0,1:T(1,128)}, u32[]{:S(2)}) copy-start(f32[1,3,1920]{2,0,1:T(1,128)} %get-tuple-element.21) | copy-start | bytes 69124
  137.1 10.1 %all-to-all-start.3 = ((bf16[8,25,240]{2,1,0:T(8,128)(2,1)}), bf16[8,25,240]{2,1,0:T(8,128)(2,1)S(1)}, u32[]{:S(2)}, u32[]{:S(2)}) async-start(bf16[8,25,240]{2,1,0:T(8,128)(2,1)} %convolution_convert_fusion.5), calls=%async_computation.3 | async-start | bytes 262144 | tf_op jit(solution)/shard_map/all_to_all | solution.py:192
  147.3 27.7 %copy-start.6 = (f32[1,25,8,240]{3,2,0,1:T(8,128)}, f32[1,25,8,240]{3,2,0,1:T(8,128)S(1)}, u32[]{:S(2)}) copy-start(f32[1,25,8,240]{3,2,0,1:T(8,128)S(1)} %copy.178) | copy-start | bytes 576004
  147.6 7.7 %collective-permute-start = (bf16[1,25,1920]{2,1,0:T(8,128)(2,1)S(1)}, bf16[1,25,1920]{2,1,0:T(8,128)(2,1)S(1)}, u32[]{:S(2)}, u32[]{:S(2)}) collective-permute-start(bf16[1,25,1920]{2,1,0:T(8,128)(2,1)S(1)} %fusion.46), channel_id=1, source_target_pairs={{0,8},{8,16},{16,24},{1,9},{9,17},{17,25},{2,10},{10,18},{18,26},{... | collective-permute-start | bytes 288008 | tf_op jit(solution)/shard_map/ppermute | solution.py:15
  175.0 12.6 %copy-start.10 = (bf16[30,1920]{1,0:T(8,128)(2,1)S(1)}, bf16[30,1920]{1,0:T(8,128)(2,1)}, u32[]{:S(2)}) copy-start(bf16[30,1920]{1,0:T(8,128)(2,1)} %get-tuple-element.7) | copy-start | bytes 345604
  179.2 16.6 %all-to-all-start.4 = ((bf16[8,25,3,240]{3,1,2,0:T(8,128)(2,1)}), bf16[8,25,3,240]{3,1,2,0:T(8,128)(2,1)}, u32[]{:S(2)}, u32[]{:S(2)}) async-start(bf16[8,25,3,240]{3,1,2,0:T(8,128)(2,1)} %copy.187), calls=%async_computation.4 | async-start | bytes 786432 | tf_op jit(solution)/shard_map/all_to_all | solution.py:74
  199.2 9.7 %copy-start.2 = (bf16[1,25,3,1920]{3,1,2,0:T(8,128)(2,1)}, bf16[1,25,3,1920]{3,1,2,0:T(8,128)(2,1)S(1)}, u32[]{:S(2)}) copy-start(bf16[1,25,3,1920]{3,1,2,0:T(8,128)(2,1)S(1)} %all_to_all.72) | copy-start | bytes 864004
  209.5 7.1 %slice-start.1 = ((bf16[1,25,3,1920]{3,1,2,0:T(8,128)(2,1)}), bf16[1,25,1,1920]{3,1,2,0:T(8,128)(2,1)S(1)}, s32[]{:S(2)}) async-start(bf16[1,25,3,1920]{3,1,2,0:T(8,128)(2,1)} %copy-done.2), calls=%async_computation.8 | async-start | bytes 245760 | tf_op jit(solution)/shard_map/slice | solution.py:80
  215.5 0.8 copy-start.5
  217.6 12.0 %copy-start.7 = (f32[1,25,8,240]{3,2,0,1:T(8,128)S(1)}, f32[1,25,8,240]{3,2,0,1:T(8,128)}, u32[]{:S(2)}) copy-start(f32[1,25,8,240]{3,2,0,1:T(8,128)} %copy-done.6) | copy-start | bytes 576004
  225.3 29.4 %all-to-all-start.5 = ((bf16[8,1,25,1920]{3,2,1,0:T(8,128)(2,1)}), bf16[8,1,25,1920]{3,2,1,0:T(8,128)(2,1)}, u32[]{:S(2)}, u32[]{:S(2)}) async-start(bf16[8,1,25,1920]{3,2,1,0:T(8,128)(2,1)} %stack.12), calls=%async_computation.5 | async-start | bytes 1966080 | tf_op jit(solution)/shard_map/all_to_all | solution.py:108
  257.3 10.8 %all-to-all-start.6 = ((bf16[8,25,240]{2,1,0:T(8,128)(2,1)}), bf16[8,25,240]{2,1,0:T(8,128)(2,1)}, u32[]{:S(2)}, u32[]{:S(2)}) async-start(bf16[8,25,240]{2,1,0:T(8,128)(2,1)} %convolution_convert_fusion.4), calls=%async_computation.6 | async-start | bytes 262144 | tf_op jit(solution)/shard_map/all_to_all | solution.py:192
